TPU v7x, 512 devices: a whole 4x8x8 slice. The times are simulated.
512 devices in a mesh: dp: 4 (over x), expert: 128 (over z, y, core).
Axes of the slice: x: 4, y: 8, z: 8, core: 2. Of those that a mesh axis runs over, the one named last changes fastest.
Arguments:
- expert_down: bfloat16 [49152, 2048], P('expert'), may hold values from -0.125 to 0.125
- out_grad: bfloat16 [65536, 2048], P(('dp', 'expert')), parts along dimension 0, may hold values from -6 to 6
- routes: int32 [65536, 8], P(('dp', 'expert')), parts along dimension 0, may hold values from 0 to 63, all different within a row; in each aligned block of 128 rows (0 to 127, 128 to 255, ...) at most 24 rows name the same one
- gates: float32 [65536, 8], P(('dp', 'expert')), parts along dimension 0, may hold values from 0.1 to 1
Outputs:
- hidden_grad: bfloat16 [65536, 8, 768], P(('dp', 'expert')), parts along dimension 0
There are 4 independent parts, one for each index of `dp`. A program takes and returns all parts, laid end to end along the dimension named above; an argument that names none is the same for every part. Nothing has to cross between parts.
Inputs may be any that keep to these rules, and one draw needn't show every extreme that they name: `routes`: each token names 8 different experts; among the 128 tokens of one device no expert is named more than 24 times.
All inputs are finite; a program needn't handle non-finite values.
Results may differ from a plain program's by a relative error of at most 0.0049.
Values may be sent and summed in bfloat16 or wider, within the bound.
A program may use at most 64 MiB of HBM per device.

v0:
```python
import jax
import jax.numpy as jnp
from jax import lax
from jax.sharding import PartitionSpec as P


def swapped(value, axis, apart):
    mask = 2**apart
    pairs = [(source, source ^ mask) for source in range(lax.axis_size(axis))]
    return lax.ppermute(value, axis, pairs)


def slot_table(routes, experts, capacity):
    local_tokens, choices = routes.shape
    expert_ids = routes.reshape(-1)
    one_hot = (expert_ids[:, None] == jnp.arange(experts, dtype=jnp.int32)[None, :]).astype(
        jnp.int32
    )
    earlier = jnp.cumsum(one_hot, axis=0) - one_hot
    slots = jnp.sum(earlier * one_hot, axis=1)
    position = expert_ids * capacity + slots
    source_token = jnp.arange(local_tokens * choices, dtype=jnp.int32) // choices
    token_table = jnp.zeros((experts * capacity,), jnp.int32).at[position].set(source_token)
    return (expert_ids, slots, token_table.reshape(experts, capacity))


def contract_width(rows, weight):
    return lax.dot_general(
        rows, weight, (((2,), (1,)), ((), ())), preferred_element_type=jnp.float32
    )


def shards(expert_down, out_grad, routes, gates):
    devices = lax.axis_size("expert")
    experts = devices // 2
    local_tokens, choices = routes.shape
    model_width = out_grad.shape[1]
    hidden_half = expert_down.shape[0]
    capacity = 3 * local_tokens * choices // (2 * experts)
    expert_ids, slots, token_table = slot_table(routes, experts, capacity)
    parity = lax.axis_index("expert") % 2
    width_half = model_width // 2
    split_grad = out_grad.reshape(local_tokens, 2, width_half).transpose(1, 0, 2)
    outgoing = split_grad[jnp.arange(2, dtype=jnp.int32)[None, :, None], token_table[:, None, :]]
    outgoing = outgoing.reshape(devices, capacity, width_half)
    own_columns = lax.dynamic_slice_in_dim(expert_down, parity * width_half, width_half, 1)
    partner_columns = lax.dynamic_slice_in_dim(
        expert_down, (1 - parity) * width_half, width_half, 1
    )
    arrived = lax.all_to_all(outgoing, "expert", split_axis=0, concat_axis=0, tiled=True)
    partner = swapped(arrived, "expert", 0)
    product = contract_width(arrived, own_columns) + contract_width(partner, partner_columns)
    returned = lax.all_to_all(
        product.astype(jnp.bfloat16), "expert", split_axis=0, concat_axis=0, tiled=True
    )
    picked = returned.reshape(experts, 2, capacity, hidden_half)[expert_ids, :, slots, :]
    picked = picked.reshape(local_tokens * choices, 2 * hidden_half)
    result = (gates.reshape(-1)[:, None] * picked.astype(jnp.float32)).astype(jnp.bfloat16)
    return result.reshape(local_tokens, choices, 2 * hidden_half)


def solution(mesh):
    placed = (
        P("expert", None),
        P(("dp", "expert"), None),
        P(("dp", "expert"), None),
        P(("dp", "expert"), None),
    )
    return jax.shard_map(
        shards,
        mesh=mesh,
        in_specs=placed,
        out_specs=P(("dp", "expert"), None, None),
        check_vma=False,
    )
```

profile of v0, /device:TPU:1, one launch (start us, length us, event | category | flops | bytes accessed | tf_op | source)
XLA Modules:
  0.0 353.4 jit_solution(12502992809371012809)
XLA Ops:
  0.0 0.0 copy-start
  0.0 0.9 copy.41
  0.9 0.1 eq.31
  1.0 0.1 eq.27
  1.1 0.1 reshape.129
  1.3 18.0 %reduce-window.6 = s32[64,8,128]{2,1,0:T(8,128)S(1)} reduce-window(s32[64,8,128]{2,1,0:T(8,128)S(1)} %fusion.8, s32[]{:T(128)} %constant.44.clone.1), window={size=1x1x128 pad=0_0x0_0x127_0}, to_apply=%region_0.0 | reduce-window | flops 8323072 | bytes 524292 | tf_op jit(solution)/shard_map/reduce-window
  19.3 0.1 slice.12
  19.4 0.1 copy.44
  19.6 0.1 copy.45
  19.7 0.1 broadcast_add_fusion
  19.8 0.1 fusion.7
  19.9 4.3 %scatter_custom_fusion = s32[1536]{0:T(1024)S(1)} fusion(s32[1024]{0:T(1024)S(1)} %bitcast.41, s32[1024]{0:T(1024)S(1)} %add_select_fusion, s32[]{:T(128)} %constant.44.clone.1), kind=kCustom, calls=%fused_computation.36 | custom fusion | bytes 6148 | tf_op jit(solution)/shard_map/scatter | solution.py:23
  24.3 0.1 broadcast_in_dim_reshape.2
  24.4 0.1 reshape.134
  24.5 0.0 copy-done.2
  24.5 0.3 copy.39
  24.8 0.2 copy.40
  25.0 45.0 %gather_fusion = bf16[3072,1024]{1,0:T(8,128)(2,1)} fusion(bf16[2,128,1024]{2,1,0:T(8,128)(2,1)S(1)} %bitcast.34, s32[3072]{0:T(1024)S(1)} %reshape.134), kind=kCustom, calls=%fused_computation | custom fusion | bytes 12607488 | tf_op jit(solution)/shard_map/gather | solution.py:44
  70.0 159.9 %all_to_all.10 = bf16[128,24,1024]{2,1,0:T(8,128)(2,1)S(1)} all-to-all(bf16[128,24,1024]{2,1,0:T(8,128)(2,1)} %bitcast.36), channel_id=1, replica_groups=mesh['dp'=4,'expert'=128] {'expert'}, dimensions={0} | all-to-all | bytes 12582912 | tf_op jit(solution)/shard_map/all_to_all | solution.py:50
  229.9 6.2 %copy.46 = bf16[128,24,1024]{2,0,1:T(8,128)(2,1)} copy(bf16[128,24,1024]{2,1,0:T(8,128)(2,1)S(1)} %all_to_all.10) | data formatting | bytes 12582912 | tf_op jit(solution)/shard_map/all_to_all | solution.py:50
  236.1 3.7 %collective-permute-start = (bf16[128,24,1024]{2,0,1:T(8,128)(2,1)}, bf16[128,24,1024]{2,0,1:T(8,128)(2,1)}, u32[]{:S(2)}, u32[]{:S(2)}) collective-permute-start(bf16[128,24,1024]{2,0,1:T(8,128)(2,1)} %copy.46), channel_id=1, source_target_pairs={{0,1},{1,0},{2,3},{3,2},{4,5},{5,4},{6,7},{7,6},{8,9},{9,8},{10,11... | collective-permute-start | bytes 18874376 | tf_op jit(solution)/shard_map/ppermute | solution.py:10
  239.9 8.0 %fusion.1 = f32[128,24,384]{2,0,1:T(8,128)S(1)} fusion(bf16[384,2048]{1,0:T(8,128)(2,1)S(1)} %copy-done, s32[]{:T(128)S(6)} %select_n.60, bf16[128,24,1024]{2,1,0:T(8,128)(2,1)} %copy-done.1), kind=kOutput, calls=%fused_computation.6 | convolution fusion | flops 2415919104 | bytes 11796484 | tf_op jit(solution)/shard_map/dot_general | solution.py:28
  247.9 1.9 collective-permute-done
  249.8 6.3 %add_convert_fusion = bf16[128,24,384]{2,0,1:T(8,128)(2,1)S(1)} fusion(f32[128,24,384]{2,0,1:T(8,128)S(1)} %fusion.1, bf16[128,24,1024]{2,0,1:T(8,128)(2,1)} %collective-permute-done, bf16[384,2048]{1,0:T(8,128)(2,1)S(1)} %copy-done, s32[]{:T(128)S(6)} %select_n.61), kind=kOutput, calls=%fused_computation.3 | convolution fusion | flops 2418278400 | bytes 14155780 | tf_op jit(solution)/shard_map/dot_general | solution.py:28
  256.0 2.8 copy.48
  258.8 20.3 %all-to-all-start.1 = ((bf16[128,24,384]{2,1,0:T(8,128)(2,1)}), bf16[128,24,384]{2,1,0:T(8,128)(2,1)}, u32[]{:S(2)}, u32[]{:S(2)}) async-start(bf16[128,24,384]{2,1,0:T(8,128)(2,1)} %copy.48), calls=%async_computation.1 | async-start | bytes 4718592 | tf_op jit(solution)/shard_map/all_to_all | solution.py:53
  279.1 0.1 copy.38
  279.2 56.1 %all-to-all-done.1 = bf16[128,24,384]{2,1,0:T(8,128)(2,1)} async-done(((bf16[128,24,384]{2,1,0:T(8,128)(2,1)}), bf16[128,24,384]{2,1,0:T(8,128)(2,1)}, u32[]{:S(2)}, u32[]{:S(2)}) %all-to-all-start.1) | async-done | bytes 2359328 | tf_op jit(solution)/shard_map/all_to_all | solution.py:53
  335.4 4.9 %copy.49 = bf16[64,2,24,384]{3,1,2,0:T(2,128)(2,1)} copy(bf16[64,2,24,384]{3,2,1,0:T(8,128)(2,1)} %bitcast.9) | data formatting | bytes 4718592 | tf_op jit(solution)/shard_map/reshape | solution.py:56
  340.3 7.7 %gather_fusion.1 = bf16[1024,2,384]{2,1,0:T(2,128)(2,1)S(1)} fusion(bf16[64,2,24,384]{3,1,2,0:T(2,128)(2,1)} %copy.49, s32[1024]{0:T(1024)S(1)} %bitcast.35), kind=kCustom, calls=%fused_computation.1 | custom fusion | bytes 3153920 | tf_op jit(solution)/shard_map/gather | solution.py:56
  348.0 2.1 reshape.133
  350.1 3.3 multiply_convert_fusion
  (13 shorter events, 0.1 us)
Async XLA Ops:
  0.0 239.9 %copy-start = (bf16[384,2048]{1,0:T(8,128)(2,1)S(1)}, bf16[384,2048]{1,0:T(8,128)(2,1)}, u32[]{:S(2)}) copy-start(bf16[384,2048]{1,0:T(8,128)(2,1)} %param.4) | copy-start | bytes 4718596
  0.0 24.5 %copy-start.2 = (bf16[128,2048]{1,0:T(8,128)(2,1)S(1)}, bf16[128,2048]{1,0:T(8,128)(2,1)}, u32[]{:S(2)}) copy-start(bf16[128,2048]{1,0:T(8,128)(2,1)} %param.5) | copy-start | bytes 1572868
  229.9 6.2 %copy-start.1 = (bf16[128,24,1024]{2,1,0:T(8,128)(2,1)}, bf16[128,24,1024]{2,1,0:T(8,128)(2,1)S(1)}, u32[]{:S(2)}) copy-start(bf16[128,24,1024]{2,1,0:T(8,128)(2,1)S(1)} %all_to_all.10) | copy-start | bytes 18874372
  236.1 13.7 %collective-permute-start = (bf16[128,24,1024]{2,0,1:T(8,128)(2,1)}, bf16[128,24,1024]{2,0,1:T(8,128)(2,1)}, u32[]{:S(2)}, u32[]{:S(2)}) collective-permute-start(bf16[128,24,1024]{2,0,1:T(8,128)(2,1)} %copy.46), channel_id=1, source_target_pairs={{0,1},{1,0},{2,3},{3,2},{4,5},{5,4},{6,7},{7,6},{8,9},{9,8},{10,11... | collective-permute-start | bytes 18874376 | tf_op jit(solution)/shard_map/ppermute | solution.py:10
  258.8 20.3 %copy-start.3 = (f32[128,8]{0,1:T(8,128)S(1)}, f32[128,8]{0,1:T(8,128)}, u32[]{:S(2)}) copy-start(f32[128,8]{0,1:T(8,128)} %param.7) | copy-start | bytes 12292
  258.8 76.6 %all-to-all-start.1 = ((bf16[128,24,384]{2,1,0:T(8,128)(2,1)}), bf16[128,24,384]{2,1,0:T(8,128)(2,1)}, u32[]{:S(2)}, u32[]{:S(2)}) async-start(bf16[128,24,384]{2,1,0:T(8,128)(2,1)} %copy.48), calls=%async_computation.1 | async-start | bytes 4718592 | tf_op jit(solution)/shard_map/all_to_all | solution.py:53
where the time goes:
time: 356 us; the launch traced here: 353 us
  blocking collectives  160 us (45%)
  local copies, waits for them, and re-layouts  75.4 us (21%)
  waiting for transfers between devices  58 us (16%)
  starting transfers between devices  24 us (7%)
  other arithmetic  21.6 us (6%)
  matrix products  14.3 us (4%)
    all_to_all x1, blocking collectives, shards(): lax.all_to_all(outgoing, 'expert', split_axis=0, concat_axis=0, tiled=True)  160 us
    all_to_all x1, waiting for transfers between devices, shards(): lax.all_to_all(product.astype(jnp.bfloat16), 'expert', split_axis=0, conc...  56.1 us
    gather x1, local copies, waits for them, and re-layouts, shards(): split_grad[jnp.arange(2, dtype=jnp.int32)[None, :, None], token_table[:,...  45 us
    all_to_all x1, starting transfers between devices, shards(): lax.all_to_all(product.astype(jnp.bfloat16), 'expert', split_axis=0, conc...  20.3 us
    another operation x3, other arithmetic  18.2 us
    dot_general x2, matrix products, contract_width(): lax.dot_general(rows, weight, (((2,), (1,)), ((), ())), preferred_element...  14.3 us
    gather x1, local copies, waits for them, and re-layouts, shards(): returned.reshape(experts, 2, capacity, hidden_half)[expert_ids, :, slots, :]  7.67 us
  transfers between devices with their start and end apart: 2, of which 2 were waited for; matrix products, arithmetic and copies ran while one was open for 2% of the time, Pallas kernels for 0%

commit v1 on v0

v1 whole, which is shorter than its diff:
```python
import functools

import jax
import jax.numpy as jnp
from jax import lax
from jax.experimental import pallas as pl
from jax.experimental.pallas import tpu as pltpu
from jax.sharding import PartitionSpec as P

MESH = pl.DeviceIdType.MESH
RING = 8
X_RING = 4
CAP = 24
PAIR = 2 * CAP
REL = (0, 1, 7, 2, 6, 3, 5, 4)
POS = tuple(REL.index(rel) for rel in range(RING))


def position_of(rel):
    return jnp.where(rel == 0, 0, jnp.where(rel <= 4, 2 * rel - 1, 2 * (8 - rel)))


def rel_of(position):
    half = (position + 1) >> 1
    return jnp.where(position & 1 == 1, half, (8 - half) & 7)


def kernel(
    down_ref,
    grad_ref,
    routes_ref,
    routes_t_ref,
    out_ref,
    tok,
    wts,
    rows_x,
    outgoing,
    returned,
    select,
    routes_all,
    slots_all,
    local_sem,
    tz_send,
    tz_recv,
    tp_send,
    tp_recv,
    own_send,
    own_recv,
    wy_send,
    wy_recv,
    wx_send,
    wx_recv,
    r_send,
    r_recv,
    b_send,
    b_recv,
):
    f32, bf16 = jnp.float32, jnp.bfloat16
    local_tokens, width = grad_ref.shape
    hidden = down_ref.shape[0]
    half_tok = local_tokens // 2
    quarter = hidden // 4
    x = lax.axis_index("dp")
    ex = lax.axis_index("expert")
    core = ex % 2
    other = 1 - core
    y = (ex // 2) % RING
    z = ex // (2 * RING)

    def at_z(rel, c):
        return (x, (((z + rel) % RING) * RING + y) * 2 + c)

    def at_y(rel):
        return (x, (z * RING + (y + rel) % RING) * 2 + core)

    def at_x(rel):
        return ((x + rel) % X_RING, ex)

    partner = (x, ex + 1 - 2 * core)
    pending = []

    def send(src, dst, send_sem, recv_sem, device):
        copy = pltpu.make_async_remote_copy(
            src_ref=src,
            dst_ref=dst,
            send_sem=send_sem,
            recv_sem=recv_sem,
            device_id=device,
            device_id_type=MESH,
        )
        copy.start()
        pending.append(copy)

    def await_copy(ref, sem):
        pltpu.make_async_copy(ref, ref, sem).wait()

    own_rows = pl.ds(pl.multiple_of(core * local_tokens, local_tokens), local_tokens)
    load_tok = pltpu.make_async_copy(grad_ref, tok.at[0, own_rows], local_sem.at[0])
    load_wts = pltpu.make_async_copy(down_ref, wts.at[0], local_sem.at[1])
    load_tok.start()
    load_wts.start()

    barrier = pltpu.get_barrier_semaphore()
    peers = [partner, at_y(1), at_y(-1 + RING), at_x(1), at_x(-1 + X_RING)]
    peers += [at_z(rel, c) for rel in range(1, RING) for c in range(2)]
    for peer in peers:
        pl.semaphore_signal(barrier, inc=1, device_id=peer, device_id_type=MESH)
    pl.semaphore_wait(barrier, len(peers))

    def tok_chunk(rel, half, c=None):
        c = core if c is None else c
        start = pl.multiple_of(c * local_tokens + half * half_tok, half_tok)
        return tok.at[POS[rel % RING], pl.ds(start, half_tok)]

    def z_send(direction, k):
        d = k // 2
        if direction == 0:
            half, src, dst, hop = k % 2, -d, -d - 1, 1
        else:
            half, src, dst, hop = 1 - k % 2, d, d + 1, RING - 1
        send(
            tok_chunk(src, half),
            tok_chunk(dst, half),
            tz_send.at[direction, k],
            tz_recv.at[direction, k],
            at_z(hop, core),
        )

    def z_arrival(direction, k):
        d = k // 2
        return (-d - 1, k % 2) if direction == 0 else (d + 1, 1 - k % 2)

    def z_event(k):
        for direction in range(2):
            chunk = z_arrival(direction, k)
            await_copy(tok_chunk(*chunk), tz_recv.at[direction, k])
            if k <= 4:
                z_send(direction, k + 2)
            send(
                tok_chunk(*chunk),
                tok_chunk(*chunk),
                tp_send.at[direction, k],
                tp_recv.at[direction, k],
                partner,
            )

    def partner_event(k):
        for direction in range(2):
            await_copy(tok_chunk(*z_arrival(direction, k), other), tp_recv.at[direction, k])

    base = 2 * (x % 2)

    def w_chunk(rel, part, quarters):
        start = pl.multiple_of((quarters + part) * quarter, quarter)
        return wts.at[POS[rel % RING], pl.ds(start, quarter)]

    def y_send(direction, k):
        d = k // 2
        if direction == 0:
            part, src, dst, hop = k % 2, -d, -d - 1, 1
        else:
            part, src, dst, hop = 1 - k % 2, d, d + 1, RING - 1
        send(
            w_chunk(src, part, base),
            w_chunk(dst, part, base),
            wy_send.at[direction, k],
            wy_recv.at[direction, k],
            at_y(hop),
        )

    def y_event(k):
        for direction in range(2):
            rel, part = z_arrival(direction, k)
            await_copy(w_chunk(rel, part, base), wy_recv.at[direction, k])
            if k <= 4:
                y_send(direction, k + 2)
            send(
                w_chunk(rel, part, base),
                w_chunk(rel, part, base),
                wx_send.at[part, k],
                wx_recv.at[part, k],
                at_x(X_RING - 1 if part == 0 else 1),
            )

    def x_event(k):
        for direction in range(2):
            rel, part = z_arrival(direction, k)
            await_copy(w_chunk(rel, part, 2 - base), wx_recv.at[part, k])

    def gather(q):
        slots = jnp.concatenate([slots_all[q, 0], slots_all[q, 1]], axis=1)
        number = lax.broadcasted_iota(jnp.int32, (PAIR, 2 * local_tokens), 0).astype(f32)
        pick = jnp.concatenate(
            [jnp.where(slots[p : p + 1, :] == number, 1.0, 0.0) for p in range(RING)], axis=0
        ).astype(bf16)
        cols = 512

        def body(n, carry):
            span = pl.ds(pl.multiple_of(n * cols, cols), cols)
            got = jnp.dot(pick, tok[q, :, span], preferred_element_type=f32)
            rows_x[:, q * PAIR : (q + 1) * PAIR, span] = got.astype(bf16).reshape(RING, PAIR, cols)
            return carry

        lax.fori_loop(0, width // cols, body, 0)

    def multiply(pair, first, last):
        products = []
        for p in (2 * pair, 2 * pair + 1):
            value = lax.dot_general(
                rows_x[p, first * PAIR : last * PAIR, :],
                wts[p],
                (((1,), (1,)), ((), ())),
                preferred_element_type=f32,
            )
            products.append(value.reshape(2 * (last - first), CAP, hidden))
        both = jnp.concatenate(products, axis=1).astype(bf16)
        outgoing[pair, 2 * first : 2 * last] = both

    def send_back(pair, positions):
        for q in positions:
            rel = REL[q]
            if q == 0:
                returned[core, pair, 0] = outgoing[pair, core]
                send(
                    outgoing.at[pair, other],
                    returned.at[core, pair, 0],
                    b_send.at[pair, 0, 0],
                    b_recv.at[pair, 0, 0],
                    partner,
                )
                continue
            for c in range(2):
                send(
                    outgoing.at[pair, 2 * q + c],
                    returned.at[core, pair, POS[(RING - rel) % RING]],
                    b_send.at[pair, q, c],
                    b_recv.at[pair, POS[(RING - rel) % RING], core],
                    at_z(rel, c),
                )

    def assemble(pair):
        await_copy(returned.at[other, pair, 0], b_recv.at[pair, 0, 0])
        for q in range(1, RING):
            for c in range(2):
                await_copy(returned.at[c, pair, q], b_recv.at[pair, q, c])
        rows = local_tokens

        for c in range(2):
            block = returned[c, pair].reshape(RING * PAIR, hidden)

            def body(n, carry):
                span = pl.ds(pl.multiple_of(n * rows, rows), rows)
                got = jnp.dot(
                    select[span, pair * RING * PAIR : (pair + 1) * RING * PAIR],
                    block,
                    preferred_element_type=f32,
                ).astype(bf16)
                columns = slice(c * hidden, (c + 1) * hidden)
                if pair == 0:
                    out_ref[span, columns] = got
                else:
                    out_ref[span, columns] = out_ref[span, columns] + got
                return carry

            lax.fori_loop(0, out_ref.shape[0] // rows, body, 0)

    def home_selection():
        top = routes_ref.shape[1]
        routes = routes_ref[...]
        lane = lax.broadcasted_iota(jnp.int32, (local_tokens, local_tokens), 1)
        sub = lax.broadcasted_iota(jnp.int32, (local_tokens, local_tokens), 0)
        named = jnp.zeros((local_tokens, local_tokens), f32)
        for j in range(top):
            named = jnp.where(routes[:, j : j + 1] == lane, 1.0, named)
        earlier = jnp.where(lane < sub, 1.0, 0.0).astype(bf16)
        counts = jnp.dot(earlier, named.astype(bf16), preferred_element_type=f32).astype(bf16)
        routes_b = routes.astype(f32).astype(bf16)
        p = position_of(((lane & 7) - y + RING) & 7)
        q = position_of(((lane >> 3) - z + 2 * RING) & 7)
        first = ((p >> 1) * (RING * PAIR) + q * PAIR + (p & 1) * CAP).astype(f32)
        lane_f = lane.astype(f32)
        j_lane = lax.broadcasted_iota(jnp.int32, (local_tokens, top), 1)
        j_sub = lax.broadcasted_iota(jnp.int32, (local_tokens, top), 0)
        columns = RING * PAIR
        number = lax.broadcasted_iota(jnp.int32, (local_tokens, columns), 1).astype(f32)

        def body(n, carry):
            token = n * (local_tokens // top) + (sub >> 3)
            repeat = jnp.where(token == lane, 1.0, 0.0).astype(bf16)
            chosen = jnp.dot(repeat, routes_b, preferred_element_type=f32)
            chosen = jnp.sum(jnp.where(j_lane == (j_sub & 7), chosen, 0.0), axis=1, keepdims=True)
            slot = jnp.dot(repeat, counts, preferred_element_type=f32)
            place = jnp.sum(jnp.where(lane_f == chosen, slot + first, 0.0), axis=1, keepdims=True)
            span = pl.ds(pl.multiple_of(n * local_tokens, local_tokens), local_tokens)
            for pair in range(RING // 2):
                hit = jnp.where(place == number + float(pair * columns), 1.0, 0.0)
                select[span, pair * columns : (pair + 1) * columns] = hit.astype(bf16)
            return carry

        lax.fori_loop(0, top, body, 0)

    def source_slots():
        sub = lax.broadcasted_iota(jnp.int32, (RING, local_tokens), 0)
        expert = z * RING + ((y + rel_of(sub)) & 7)
        named = []
        for q in range(RING):
            for s in range(2):
                value = jnp.zeros((RING, local_tokens), f32)
                for j in range(RING):
                    value = jnp.where(routes_all[q, s, j : j + 1, :] == expert, 1.0, value)
                named.append(value)
        named = jnp.concatenate(named, axis=0)
        a = lax.broadcasted_iota(jnp.int32, (local_tokens, local_tokens), 0)
        b = lax.broadcasted_iota(jnp.int32, (local_tokens, local_tokens), 1)
        before = jnp.where(a < b, 1.0, 0.0).astype(bf16)
        counts = jnp.dot(named.astype(bf16), before, preferred_element_type=f32)
        row = lax.broadcasted_iota(jnp.int32, named.shape, 0)
        counts = counts + jnp.where((row >> 3) & 1 == 1, float(CAP), 0.0)
        slots_all[...] = jnp.where(named > 0.5, counts, -1.0).reshape(slots_all.shape)

    load_tok.wait()
    for k in range(2):
        for direction in range(2):
            z_send(direction, k)
    for rel in range(1, RING):
        for c in range(2):
            send(
                routes_t_ref,
                routes_all.at[POS[RING - rel], core],
                r_send.at[POS[rel], c],
                r_recv.at[POS[RING - rel], core],
                at_z(rel, c),
            )
    send(routes_t_ref, routes_all.at[0, core], r_send.at[0, 0], r_recv.at[0, 0], partner)
    load_wts.wait()
    for k in range(2):
        for direction in range(2):
            y_send(direction, k)
    send(tok.at[0, own_rows], tok.at[0, own_rows], own_send, own_recv, partner)
    routes_all[0, core] = routes_t_ref[...]

    home_selection()
    await_copy(routes_all.at[0, other], r_recv.at[0, 0])
    for q in range(1, RING):
        for c in range(2):
            await_copy(routes_all.at[q, c], r_recv.at[q, c])
    source_slots()
    other_rows = pl.ds(pl.multiple_of(other * local_tokens, local_tokens), local_tokens)
    await_copy(tok.at[0, other_rows], own_recv)
    gather(0)

    z_event(0)
    y_event(0)
    z_event(1)
    partner_event(0)
    partner_event(1)
    gather(1)
    gather(2)
    y_event(1)
    z_event(2)
    x_event(0)
    z_event(3)
    partner_event(2)
    partner_event(3)
    gather(3)
    gather(4)
    y_event(2)
    z_event(4)
    x_event(1)
    y_event(3)
    z_event(5)
    partner_event(4)
    partner_event(5)
    gather(5)
    gather(6)
    multiply(0, 0, 7)
    send_back(0, (5, 6, 3, 4, 1, 2, 0))
    x_event(2)
    z_event(6)
    partner_event(6)
    gather(7)
    multiply(0, 7, 8)
    send_back(0, (7,))
    y_event(4)
    x_event(3)
    order = (7, 5, 6, 3, 4, 1, 2, 0)
    multiply(1, 0, 8)
    send_back(1, order)
    y_event(5)
    assemble(0)
    x_event(4)
    y_event(6)
    x_event(5)
    multiply(2, 0, 8)
    send_back(2, order)
    assemble(1)
    x_event(6)
    multiply(3, 0, 8)
    send_back(3, order)
    assemble(2)
    assemble(3)
    for copy in pending:
        copy.wait_send()


def shards(expert_down, out_grad, routes, gates):
    hidden, width = expert_down.shape
    local_tokens, top = routes.shape
    bf16 = jnp.bfloat16
    dma = pltpu.SemaphoreType.DMA
    picked = pl.pallas_call(
        kernel,
        out_shape=jax.ShapeDtypeStruct((local_tokens * top, 2 * hidden), bf16),
        in_specs=[pl.BlockSpec(memory_space=pl.ANY)] * 2
        + [pl.BlockSpec(memory_space=pltpu.VMEM)] * 2,
        out_specs=pl.BlockSpec(memory_space=pltpu.VMEM),
        scratch_shapes=[
            pltpu.VMEM((RING, 2 * local_tokens, width), bf16),
            pltpu.VMEM((RING, hidden, width), bf16),
            pltpu.VMEM((RING, RING * PAIR, width), bf16),
            pltpu.VMEM((RING // 2, 2 * RING, PAIR, hidden), bf16),
            pltpu.VMEM((2, RING // 2, RING, PAIR, hidden), bf16),
            pltpu.VMEM((local_tokens * top, RING * RING * CAP), bf16),
            pltpu.VMEM((RING, 2, top, local_tokens), jnp.int32),
            pltpu.VMEM((RING, 2, RING, local_tokens), jnp.float32),
            dma((2,)),
            dma((2, 7)),
            dma((2, 7)),
            dma((2, 7)),
            dma((2, 7)),
            dma(()),
            dma(()),
            dma((2, 7)),
            dma((2, 7)),
            dma((2, 7)),
            dma((2, 7)),
            dma((RING, 2)),
            dma((RING, 2)),
            dma((RING // 2, RING, 2)),
            dma((RING // 2, RING, 2)),
        ],
        compiler_params=pltpu.CompilerParams(
            collective_id=0, has_side_effects=True, vmem_limit_bytes=60 * 2**20
        ),
    )(expert_down, out_grad, routes, routes.T)
    picked = picked.reshape(local_tokens, top, 2 * hidden)
    return (gates[:, :, None] * picked.astype(jnp.float32)).astype(bf16)


def solution(mesh):
    placed = (
        P("expert", None),
        P(("dp", "expert"), None),
        P(("dp", "expert"), None),
        P(("dp", "expert"), None),
    )
    return jax.shard_map(
        shards,
        mesh=mesh,
        in_specs=placed,
        out_specs=P(("dp", "expert"), None, None),
        check_vma=False,
    )
```

time: 356 us -> 126 us (0.35)
  blocking collectives: 160 us -> 0 us
  Pallas kernels: 0 us -> 121 us
  local copies, waits for them, and re-layouts: 75.4 us -> 2.2 us
  waiting for transfers between devices: 58 us -> 0 us
  starting transfers between devices: 24 us -> 0 us
  other arithmetic: 21.6 us -> 2.87 us
  matrix products: 14.3 us -> 0 us
    all_to_all x1 -> x0, blocking collectives: 160 us -> none  [shards(): lax.all_to_all(outgoing, 'expert', split_axis=0, concat_axis=0, tiled=True)]
    pallas_call x0 -> x1, Pallas kernels: none -> 121 us  [shards(): pl.pallas_call(kernel, out_shape=jax.ShapeDtypeStruct((local_tokens * top...]
    all_to_all x1 -> x0, waiting for transfers between devices: 56.1 us -> none  [shards(): lax.all_to_all(product.astype(jnp.bfloat16), 'expert', split_axis=0, conc...]
    gather x2 -> x0, local copies, waits for them, and re-layouts: 52.7 us -> none  [the longest x1 45 us: shards(): split_grad[jnp.arange(2, dtype=jnp.int32)[None, :, None], token_table[:,...]
    all_to_all x1 -> x0, starting transfers between devices: 20.3 us -> none  [shards(): lax.all_to_all(product.astype(jnp.bfloat16), 'expert', split_axis=0, conc...]
    another operation x3 -> x0, other arithmetic: 18.2 us -> none
    dot_general x2 -> x0, matrix products: 14.3 us -> none  [contract_width(): lax.dot_general(rows, weight, (((2,), (1,)), ((), ())), preferred_element...]
    all_to_all x1 -> x0, local copies, waits for them, and re-layouts: 6.19 us -> none  [shards(): lax.all_to_all(outgoing, 'expert', split_axis=0, concat_axis=0, tiled=True)]
  transfers between devices with their start and end apart: 2 -> 0, of which waited for: 2 -> 0; matrix products, arithmetic and copies ran while one was open for 2% -> 0% of each run, Pallas kernels for 0% -> 0%
where the time goes in v1:
time: 126 us
  Pallas kernels  121 us (96%)
  other arithmetic  2.87 us (2%)
  local copies, waits for them, and re-layouts  2.2 us (2%)
    pallas_call x1, Pallas kernels, shards(): pl.pallas_call(kernel, out_shape=jax.ShapeDtypeStruct((local_tokens * top...  121 us
    convert_element_type x1, other arithmetic, shards(): return (gates[:, :, None] * picked.astype(jnp.float32)).astype(bf16)  2.87 us

profile of v1, /device:TPU:1, one launch (start us, length us, event | category | flops | bytes accessed | tf_op | source)
XLA Modules:
  0.0 125.8 jit_solution(293286692380588772)
XLA Ops:
  0.0 0.8 copy.5
  0.8 1.4 %copy.6.routes_ref = s32[128,8]{1,0:T(8,128)} copy(s32[128,8]{0,1:T(8,128)} %param.6) | data formatting | bytes 8192 | tf_op args[2]
  2.2 120.7 %shard_map.46 = bf16[1024,768]{1,0:T(8,128)(2,1)} custom-call(bf16[384,2048]{1,0:T(8,128)(2,1)} %down_ref.1, bf16[128,2048]{1,0:T(8,128)(2,1)} %grad_ref.1, s32[128,8]{1,0:T(8,128)} %copy.6.routes_ref, s32[8,128]{1,0:T(8,128)} %bitcast.4), custom_call_target="tpu_custom_call" | custom-call | tf_op jit(solution)/shard_map/pallas_call | solution.py:411
  122.9 2.9 %fusion = bf16[128,8,768]{2,1,0:T(8,128)(2,1)} fusion(bf16[1024,768]{1,0:T(8,128)(2,1)} %shard_map.46, f32[128,8]{1,0:T(8,128)S(1)} %copy.5), kind=kLoop, calls=%fused_computation.1 | loop fusion | flops 2359296 | bytes 3149824 | tf_op jit(solution)/shard_map/convert_element_type | solution.py:447

commit v2 on v1

--- a/solution.py
+++ b/solution.py
@@ -14,6 +14,8 @@
 PAIR = 2 * CAP
 REL = (0, 1, 7, 2, 6, 3, 5, 4)
 POS = tuple(REL.index(rel) for rel in range(RING))
+GROUPS = ((0, 1), (2, 3), (4,), (5, 6), (7,))
+STARTS = tuple(sum(len(g) for g in GROUPS[:n]) * RING * CAP for n in range(len(GROUPS)))
 
 
 def position_of(rel):
@@ -28,14 +30,24 @@
 def kernel(
     down_ref,
     grad_ref,
-    routes_ref,
     routes_t_ref,
+    gates_t_ref,
     out_ref,
+    returned_4,
+    select_4,
+    scale,
     tok,
     wts,
     rows_x,
-    outgoing,
-    returned,
+    outgoing_0,
+    outgoing_1,
+    outgoing_2,
+    outgoing_3,
+    outgoing_4,
+    returned_0,
+    returned_1,
+    returned_2,
+    returned_3,
     select,
     routes_all,
     slots_all,
@@ -56,6 +68,8 @@
     b_recv,
 ):
     f32, bf16 = jnp.float32, jnp.bfloat16
+    outgoing = (outgoing_0, outgoing_1, outgoing_2, outgoing_3, outgoing_4)
+    returned = (returned_0, returned_1, returned_2, returned_3, returned_4)
     local_tokens, width = grad_ref.shape
     hidden = down_ref.shape[0]
     half_tok = local_tokens // 2
@@ -203,9 +217,9 @@
 
         lax.fori_loop(0, width // cols, body, 0)
 
-    def multiply(pair, first, last):
+    def multiply(group, first, last):
         products = []
-        for p in (2 * pair, 2 * pair + 1):
+        for p in GROUPS[group]:
             value = lax.dot_general(
                 rows_x[p, first * PAIR : last * PAIR, :],
                 wts[p],
@@ -213,88 +227,108 @@
                 preferred_element_type=f32,
             )
             products.append(value.reshape(2 * (last - first), CAP, hidden))
-        both = jnp.concatenate(products, axis=1).astype(bf16)
-        outgoing[pair, 2 * first : 2 * last] = both
-
-    def send_back(pair, positions):
+        both = jnp.concatenate(products, axis=1) if len(products) > 1 else products[0]
+        outgoing[group][2 * first : 2 * last] = both.astype(bf16)
+
+    def send_back(group, positions):
         for q in positions:
             rel = REL[q]
             if q == 0:
-                returned[core, pair, 0] = outgoing[pair, core]
+                returned[group][core, 0] = outgoing[group][core]
                 send(
-                    outgoing.at[pair, other],
-                    returned.at[core, pair, 0],
-                    b_send.at[pair, 0, 0],
-                    b_recv.at[pair, 0, 0],
+                    outgoing[group].at[other],
+                    returned[group].at[core, 0],
+                    b_send.at[group, 0, 0],
+                    b_recv.at[group, 0, 0],
                     partner,
                 )
                 continue
             for c in range(2):
                 send(
-                    outgoing.at[pair, 2 * q + c],
-                    returned.at[core, pair, POS[(RING - rel) % RING]],
-                    b_send.at[pair, q, c],
-                    b_recv.at[pair, POS[(RING - rel) % RING], core],
+                    outgoing[group].at[2 * q + c],
+                    returned[group].at[core, POS[(RING - rel) % RING]],
+                    b_send.at[group, q, c],
+                    b_recv.at[group, POS[(RING - rel) % RING], core],
                     at_z(rel, c),
                 )
 
-    def assemble(pair):
-        await_copy(returned.at[other, pair, 0], b_recv.at[pair, 0, 0])
+    def await_returned(group):
+        await_copy(returned[group].at[other, 0], b_recv.at[group, 0, 0])
         for q in range(1, RING):
             for c in range(2):
-                await_copy(returned.at[c, pair, q], b_recv.at[pair, q, c])
-        rows = local_tokens
+                await_copy(returned[group].at[c, q], b_recv.at[group, q, c])
+
+    def assemble(group):
+        await_returned(group)
+        rows = 4 * local_tokens
+        depth = len(GROUPS[group]) * RING * CAP
 
         for c in range(2):
-            block = returned[c, pair].reshape(RING * PAIR, hidden)
 
             def body(n, carry):
                 span = pl.ds(pl.multiple_of(n * rows, rows), rows)
                 got = jnp.dot(
-                    select[span, pair * RING * PAIR : (pair + 1) * RING * PAIR],
-                    block,
+                    select[span, STARTS[group] : STARTS[group] + depth],
+                    returned[group][c].reshape(depth, hidden),
                     preferred_element_type=f32,
-                ).astype(bf16)
-                columns = slice(c * hidden, (c + 1) * hidden)
-                if pair == 0:
-                    out_ref[span, columns] = got
-                else:
-                    out_ref[span, columns] = out_ref[span, columns] + got
+                )
+                factor = scale[span, :]
+                for col in range(0, hidden, 128):
+                    columns = slice(c * hidden + col, c * hidden + col + 128)
+                    term = (factor * got[:, col : col + 128]).astype(bf16)
+                    if group == 0:
+                        out_ref[span, columns] = term
+                    else:
+                        out_ref[span, columns] = out_ref[span, columns] + term
                 return carry
 
             lax.fori_loop(0, out_ref.shape[0] // rows, body, 0)
 
     def home_selection():
-        top = routes_ref.shape[1]
-        routes = routes_ref[...]
+        top = routes_t_ref.shape[0]
+        routes = routes_t_ref[...]
         lane = lax.broadcasted_iota(jnp.int32, (local_tokens, local_tokens), 1)
         sub = lax.broadcasted_iota(jnp.int32, (local_tokens, local_tokens), 0)
-        named = jnp.zeros((local_tokens, local_tokens), f32)
+        expert_by_token = jnp.zeros((local_tokens, local_tokens), f32)
         for j in range(top):
-            named = jnp.where(routes[:, j : j + 1] == lane, 1.0, named)
+            expert_by_token = jnp.where(routes[j : j + 1, :] == sub, 1.0, expert_by_token)
         earlier = jnp.where(lane < sub, 1.0, 0.0).astype(bf16)
-        counts = jnp.dot(earlier, named.astype(bf16), preferred_element_type=f32).astype(bf16)
-        routes_b = routes.astype(f32).astype(bf16)
+        counts = lax.dot_general(
+            earlier,
+            expert_by_token.astype(bf16),
+            (((1,), (1,)), ((), ())),
+            preferred_element_type=f32,
+        ).astype(bf16)
         p = position_of(((lane & 7) - y + RING) & 7)
         q = position_of(((lane >> 3) - z + 2 * RING) & 7)
-        first = ((p >> 1) * (RING * PAIR) + q * PAIR + (p & 1) * CAP).astype(f32)
+        first = jnp.zeros(lane.shape, jnp.int32)
+        for start, group in zip(STARTS, GROUPS):
+            for n, member in enumerate(group):
+                row = start + q * (len(group) * CAP) + n * CAP
+                first = jnp.where(p == member, row, first)
+        first = first.astype(f32)
         lane_f = lane.astype(f32)
-        j_lane = lax.broadcasted_iota(jnp.int32, (local_tokens, top), 1)
-        j_sub = lax.broadcasted_iota(jnp.int32, (local_tokens, top), 0)
         columns = RING * PAIR
         number = lax.broadcasted_iota(jnp.int32, (local_tokens, columns), 1).astype(f32)
+        per_step = local_tokens // top
+        routes_rows = jnp.concatenate([routes.astype(f32)] * per_step, axis=0)
+        gates_rows = jnp.concatenate([gates_t_ref[...]] * per_step, axis=0)
 
         def body(n, carry):
-            token = n * (local_tokens // top) + (sub >> 3)
-            repeat = jnp.where(token == lane, 1.0, 0.0).astype(bf16)
-            chosen = jnp.dot(repeat, routes_b, preferred_element_type=f32)
-            chosen = jnp.sum(jnp.where(j_lane == (j_sub & 7), chosen, 0.0), axis=1, keepdims=True)
+            here = n * per_step + (sub >> 3) == lane
+            repeat = jnp.where(here, 1.0, 0.0).astype(bf16)
+            chosen = jnp.sum(jnp.where(here, routes_rows, 0.0), axis=1, keepdims=True)
+            gate = jnp.sum(jnp.where(here, gates_rows, 0.0), axis=1, keepdims=True)
             slot = jnp.dot(repeat, counts, preferred_element_type=f32)
             place = jnp.sum(jnp.where(lane_f == chosen, slot + first, 0.0), axis=1, keepdims=True)
             span = pl.ds(pl.multiple_of(n * local_tokens, local_tokens), local_tokens)
-            for pair in range(RING // 2):
-                hit = jnp.where(place == number + float(pair * columns), 1.0, 0.0)
-                select[span, pair * columns : (pair + 1) * columns] = hit.astype(bf16)
+            scale[span, :] = jnp.broadcast_to(gate, (local_tokens, scale.shape[1]))
+            for start in range(0, STARTS[-1], columns):
+                size = min(columns, STARTS[-1] - start)
+                hit = jnp.where(place == number[:, :size] + float(start), 1.0, 0.0)
+                select[span, start : start + size] = hit.astype(bf16)
+            last = jnp.where(place == number[:, : select_4.shape[1]] + float(STARTS[-1]), 1.0, 0.0)
+            select_4[span, :] = last.astype(bf16)
             return carry
 
         lax.fori_loop(0, top, body, 0)
@@ -318,11 +352,7 @@
         counts = counts + jnp.where((row >> 3) & 1 == 1, float(CAP), 0.0)
         slots_all[...] = jnp.where(named > 0.5, counts, -1.0).reshape(slots_all.shape)
 
-    load_tok.wait()
-    for k in range(2):
-        for direction in range(2):
-            z_send(direction, k)
-    for rel in range(1, RING):
+    for rel in (4, 3, 5, 2, 6, 1, 7):
         for c in range(2):
             send(
                 routes_t_ref,
@@ -332,6 +362,10 @@
                 at_z(rel, c),
             )
     send(routes_t_ref, routes_all.at[0, core], r_send.at[0, 0], r_recv.at[0, 0], partner)
+    load_tok.wait()
+    for k in range(2):
+        for direction in range(2):
+            z_send(direction, k)
     load_wts.wait()
     for k in range(2):
         for direction in range(2):
@@ -347,80 +381,113 @@
     source_slots()
     other_rows = pl.ds(pl.multiple_of(other * local_tokens, local_tokens), local_tokens)
     await_copy(tok.at[0, other_rows], own_recv)
+    z_event(0)
     gather(0)
-
-    z_event(0)
     y_event(0)
     z_event(1)
     partner_event(0)
     partner_event(1)
     gather(1)
     gather(2)
+    z_event(2)
     y_event(1)
-    z_event(2)
-    x_event(0)
     z_event(3)
     partner_event(2)
     partner_event(3)
     gather(3)
+    y_event(2)
     gather(4)
-    y_event(2)
     z_event(4)
-    x_event(1)
+    z_event(5)
     y_event(3)
-    z_event(5)
     partner_event(4)
     partner_event(5)
     gather(5)
     gather(6)
+    x_event(0)
+    x_event(1)
     multiply(0, 0, 7)
     send_back(0, (5, 6, 3, 4, 1, 2, 0))
-    x_event(2)
     z_event(6)
     partner_event(6)
     gather(7)
     multiply(0, 7, 8)
     send_back(0, (7,))
     y_event(4)
+    order = (7, 5, 6, 3, 4, 1, 2, 0)
+    x_event(2)
     x_event(3)
-    order = (7, 5, 6, 3, 4, 1, 2, 0)
     multiply(1, 0, 8)
     send_back(1, order)
+    multiply(2, 0, 8)
+    send_back(2, order)
     y_event(5)
     assemble(0)
+    y_event(6)
     x_event(4)
-    y_event(6)
     x_event(5)
-    multiply(2, 0, 8)
-    send_back(2, order)
+    multiply(3, 0, 8)
+    send_back(3, order)
     assemble(1)
     x_event(6)
-    multiply(3, 0, 8)
-    send_back(3, order)
+    multiply(4, 0, 8)
+    send_back(4, order)
     assemble(2)
     assemble(3)
+    await_returned(4)
     for copy in pending:
         copy.wait_send()
+
+
+def finish_kernel(out_ref, returned_4, select_4, scale, final_ref, buffer, sems):
+    f32, bf16 = jnp.float32, jnp.bfloat16
+    hidden = returned_4.shape[-1]
+    rows = buffer.shape[1]
+    steps = buffer.shape[0]
+    blocks = [returned_4[c].reshape(RING * CAP, hidden) for c in range(2)]
+    copies = []
+    for n in range(steps):
+        span = slice(n * rows, (n + 1) * rows)
+        factor = scale[span, :]
+        for c in range(2):
+            got = jnp.dot(select_4[span, :], blocks[c], preferred_element_type=f32)
+            for col in range(0, hidden, 128):
+                columns = slice(c * hidden + col, c * hidden + col + 128)
+                term = (factor * got[:, col : col + 128]).astype(bf16)
+                buffer[n, :, columns] = out_ref[span, columns] + term
+        copies.append(pltpu.make_async_copy(buffer.at[n], final_ref.at[span], sems.at[n]))
+        if n > 0:
+            copies[n - 1].start()
+    copies[-1].start()
+    for copy in copies:
+        copy.wait()
 
 
 def shards(expert_down, out_grad, routes, gates):
     hidden, width = expert_down.shape
     local_tokens, top = routes.shape
+    choices = local_tokens * top
     bf16 = jnp.bfloat16
     dma = pltpu.SemaphoreType.DMA
-    picked = pl.pallas_call(
+    vmem = pl.BlockSpec(memory_space=pltpu.VMEM)
+    hbm = pl.BlockSpec(memory_space=pl.ANY)
+    parts = pl.pallas_call(
         kernel,
-        out_shape=jax.ShapeDtypeStruct((local_tokens * top, 2 * hidden), bf16),
-        in_specs=[pl.BlockSpec(memory_space=pl.ANY)] * 2
-        + [pl.BlockSpec(memory_space=pltpu.VMEM)] * 2,
-        out_specs=pl.BlockSpec(memory_space=pltpu.VMEM),
+        out_shape=(
+            pltpu.VMEM((choices, 2 * hidden), bf16),
+            pltpu.VMEM((2, RING, CAP, hidden), bf16),
+            pltpu.VMEM((choices, RING * CAP), bf16),
+            pltpu.VMEM((choices, 128), jnp.float32),
+        ),
+        in_specs=[hbm, hbm, vmem, vmem],
+        out_specs=[vmem] * 4,
         scratch_shapes=[
             pltpu.VMEM((RING, 2 * local_tokens, width), bf16),
             pltpu.VMEM((RING, hidden, width), bf16),
             pltpu.VMEM((RING, RING * PAIR, width), bf16),
-            pltpu.VMEM((RING // 2, 2 * RING, PAIR, hidden), bf16),
-            pltpu.VMEM((2, RING // 2, RING, PAIR, hidden), bf16),
-            pltpu.VMEM((local_tokens * top, RING * RING * CAP), bf16),
+            *[pltpu.VMEM((2 * RING, len(g) * CAP, hidden), bf16) for g in GROUPS],
+            *[pltpu.VMEM((2, RING, len(g) * CAP, hidden), bf16) for g in GROUPS[:-1]],
+            pltpu.VMEM((choices, STARTS[-1]), bf16),
             pltpu.VMEM((RING, 2, top, local_tokens), jnp.int32),
             pltpu.VMEM((RING, 2, RING, local_tokens), jnp.float32),
             dma((2,)),
@@ -436,15 +503,26 @@
             dma((2, 7)),
             dma((RING, 2)),
             dma((RING, 2)),
-            dma((RING // 2, RING, 2)),
-            dma((RING // 2, RING, 2)),
+            dma((len(GROUPS), RING, 2)),
+            dma((len(GROUPS), RING, 2)),
         ],
         compiler_params=pltpu.CompilerParams(
-            collective_id=0, has_side_effects=True, vmem_limit_bytes=60 * 2**20
+            collective_id=0, has_side_effects=True, vmem_limit_bytes=52 * 2**20
         ),
-    )(expert_down, out_grad, routes, routes.T)
-    picked = picked.reshape(local_tokens, top, 2 * hidden)
-    return (gates[:, :, None] * picked.astype(jnp.float32)).astype(bf16)
+    )(expert_down, out_grad, routes.T, gates.T)
+    steps = 8
+    final = pl.pallas_call(
+        finish_kernel,
+        out_shape=jax.ShapeDtypeStruct((choices, 2 * hidden), bf16),
+        in_specs=[vmem] * 4,
+        out_specs=hbm,
+        scratch_shapes=[
+            pltpu.VMEM((steps, choices // steps, 2 * hidden), bf16),
+            dma((steps,)),
+        ],
+        compiler_params=pltpu.CompilerParams(vmem_limit_bytes=16 * 2**20),
+    )(*parts)
+    return final.reshape(local_tokens, top, 2 * hidden)
 
 
 def solution(mesh):

time: 126 us -> 113 us (0.90)
  Pallas kernels: 121 us -> 113 us
  other arithmetic: 2.87 us -> 0 us
  local copies, waits for them, and re-layouts: 2.2 us -> 0 us
    pallas_call x1 -> x2, Pallas kernels: 121 us -> 113 us  [the longest x1 112 us: shards(): pl.pallas_call(kernel, out_shape=(pltpu.VMEM((choices, 2 * hidden), bf16)...]
    convert_element_type x1 -> x0, other arithmetic: 2.87 us -> none  [shards(): return (gates[:, :, None] * picked.astype(jnp.float32)).astype(bf16)]
    unnamed x2 -> x0, local copies, waits for them, and re-layouts: 2.2 us -> none
where the time goes in v2:
time: 113 us
  Pallas kernels  113 us (100%)
    pallas_call x1, Pallas kernels, shards(): pl.pallas_call(kernel, out_shape=(pltpu.VMEM((choices, 2 * hidden), bf16)...  112 us

profile of v2, /device:TPU:1, one launch (start us, length us, event | category | flops | bytes accessed | tf_op | source)
XLA Modules:
  0.0 113.2 jit_solution(5884483013517375178)
XLA Ops:
  0.0 111.7 %shard_map.46 = (bf16[1024,768]{1,0:T(8,128)(2,1)S(1)}, bf16[2,8,24,384]{3,2,1,0:T(8,128)(2,1)S(1)}, bf16[1024,192]{1,0:T(8,128)(2,1)S(1)}, f32[1024,128]{1,0:T(8,128)S(1)}) custom-call(bf16[384,2048]{1,0:T(8,128)(2,1)} %down_ref.1, bf16[128,2048]{1,0:T(8,128)(2,1)} %grad_ref.1, s32[8,128]{1,0:T(8,128)} %bitcast.3, f32[8,128]{1,0:T(8,128)} %bitcast.4), custom_call_target="tpu_custom_call" | custom-call | tf_op jit(solution)/shard_map/pallas_call | solution.py:474
  111.7 1.5 %shard_map.47 = bf16[1024,768]{1,0:T(8,128)(2,1)} custom-call(bf16[1024,768]{1,0:T(8,128)(2,1)S(1)} %get-tuple-element.9.out_ref, bf16[2,8,24,384]{3,2,1,0:T(8,128)(2,1)S(1)} %get-tuple-element.10.returned_4, bf16[1024,192]{1,0:T(8,128)(2,1)S(1)} %get-tuple-element.11.select_4, f32[1024,128]{1,0:T(8,128)S(1)} %get-tuple-element.12.scale), custom_call_target="tpu_custom_call" | custom-call | tf_op jit(solution)/shard_map/pallas_call | solution.py:514

commit v3 on v2

--- a/solution.py
+++ b/solution.py
@@ -56,7 +56,6 @@
     tz_recv,
     tp_send,
     tp_recv,
-    own_send,
     own_recv,
     wy_send,
     wy_recv,
@@ -64,8 +63,12 @@
     wx_recv,
     r_send,
     r_recv,
+    rp_send,
+    rp_recv,
     b_send,
     b_recv,
+    bp_send,
+    bp_recv,
 ):
     f32, bf16 = jnp.float32, jnp.bfloat16
     outgoing = (outgoing_0, outgoing_1, outgoing_2, outgoing_3, outgoing_4)
@@ -91,7 +94,6 @@
         return ((x + rel) % X_RING, ex)
 
     partner = (x, ex + 1 - 2 * core)
-    pending = []
 
     def send(src, dst, send_sem, recv_sem, device):
         copy = pltpu.make_async_remote_copy(
@@ -103,7 +105,6 @@
             device_id_type=MESH,
         )
         copy.start()
-        pending.append(copy)
 
     def await_copy(ref, sem):
         pltpu.make_async_copy(ref, ref, sem).wait()
@@ -135,7 +136,7 @@
         send(
             tok_chunk(src, half),
             tok_chunk(dst, half),
-            tz_send.at[direction, k],
+            tz_send,
             tz_recv.at[direction, k],
             at_z(hop, core),
         )
@@ -153,7 +154,7 @@
             send(
                 tok_chunk(*chunk),
                 tok_chunk(*chunk),
-                tp_send.at[direction, k],
+                tp_send,
                 tp_recv.at[direction, k],
                 partner,
             )
@@ -177,7 +178,7 @@
         send(
             w_chunk(src, part, base),
             w_chunk(dst, part, base),
-            wy_send.at[direction, k],
+            wy_send,
             wy_recv.at[direction, k],
             at_y(hop),
         )
@@ -191,7 +192,7 @@
             send(
                 w_chunk(rel, part, base),
                 w_chunk(rel, part, base),
-                wx_send.at[part, k],
+                wx_send,
                 wx_recv.at[part, k],
                 at_x(X_RING - 1 if part == 0 else 1),
             )
@@ -238,8 +239,8 @@
                 send(
                     outgoing[group].at[other],
                     returned[group].at[core, 0],
-                    b_send.at[group, 0, 0],
-                    b_recv.at[group, 0, 0],
+                    bp_send.at[group],
+                    bp_recv.at[group],
                     partner,
                 )
                 continue
@@ -247,16 +248,14 @@
                 send(
                     outgoing[group].at[2 * q + c],
                     returned[group].at[core, POS[(RING - rel) % RING]],
-                    b_send.at[group, q, c],
-                    b_recv.at[group, POS[(RING - rel) % RING], core],
+                    b_send.at[group],
+                    b_recv.at[group],
                     at_z(rel, c),
                 )
 
     def await_returned(group):
-        await_copy(returned[group].at[other, 0], b_recv.at[group, 0, 0])
-        for q in range(1, RING):
-            for c in range(2):
-                await_copy(returned[group].at[c, q], b_recv.at[group, q, c])
+        await_copy(returned[group].at[other, 0], bp_recv.at[group])
+        await_copy(returned[group].at[:, 1:RING], b_recv.at[group])
 
     def assemble(group):
         await_returned(group)
@@ -357,11 +356,11 @@
             send(
                 routes_t_ref,
                 routes_all.at[POS[RING - rel], core],
-                r_send.at[POS[rel], c],
-                r_recv.at[POS[RING - rel], core],
+                r_send,
+                r_recv,
                 at_z(rel, c),
             )
-    send(routes_t_ref, routes_all.at[0, core], r_send.at[0, 0], r_recv.at[0, 0], partner)
+    send(routes_t_ref, routes_all.at[0, core], rp_send, rp_recv, partner)
     load_tok.wait()
     for k in range(2):
         for direction in range(2):
@@ -370,14 +369,12 @@
     for k in range(2):
         for direction in range(2):
             y_send(direction, k)
-    send(tok.at[0, own_rows], tok.at[0, own_rows], own_send, own_recv, partner)
+    send(tok.at[0, own_rows], tok.at[0, own_rows], tp_send, own_recv, partner)
     routes_all[0, core] = routes_t_ref[...]
 
     home_selection()
-    await_copy(routes_all.at[0, other], r_recv.at[0, 0])
-    for q in range(1, RING):
-        for c in range(2):
-            await_copy(routes_all.at[q, c], r_recv.at[q, c])
+    await_copy(routes_all.at[0, other], rp_recv)
+    await_copy(routes_all.at[1:RING], r_recv)
     source_slots()
     other_rows = pl.ds(pl.multiple_of(other * local_tokens, local_tokens), local_tokens)
     await_copy(tok.at[0, other_rows], own_recv)
@@ -398,16 +395,18 @@
     y_event(2)
     gather(4)
     z_event(4)
+    x_event(0)
+    x_event(1)
     z_event(5)
     y_event(3)
+    multiply(0, 0, 5)
+    send_back(0, (3, 4, 1, 2, 0))
     partner_event(4)
     partner_event(5)
     gather(5)
     gather(6)
-    x_event(0)
-    x_event(1)
-    multiply(0, 0, 7)
-    send_back(0, (5, 6, 3, 4, 1, 2, 0))
+    multiply(0, 5, 7)
+    send_back(0, (5, 6))
     z_event(6)
     partner_event(6)
     gather(7)
@@ -422,9 +421,9 @@
     multiply(2, 0, 8)
     send_back(2, order)
     y_event(5)
-    assemble(0)
     y_event(6)
     x_event(4)
+    assemble(0)
     x_event(5)
     multiply(3, 0, 8)
     send_back(3, order)
@@ -435,8 +434,15 @@
     assemble(2)
     assemble(3)
     await_returned(4)
-    for copy in pending:
-        copy.wait_send()
+    await_copy(tok.at[0 : RING - 1, 0:local_tokens], tz_send)
+    await_copy(tok.at[:, 0:local_tokens], tp_send)
+    await_copy(wts.at[0 : RING - 1, 0 : hidden // 2], wy_send)
+    await_copy(wts.at[0 : RING - 1, 0 : hidden // 2], wx_send)
+    await_copy(routes_all.at[1:RING], r_send)
+    await_copy(routes_all.at[0, other], rp_send)
+    for group in range(len(GROUPS)):
+        await_copy(outgoing[group].at[2 : 2 * RING], b_send.at[group])
+        await_copy(outgoing[group].at[other], bp_send.at[group])
 
 
 def finish_kernel(out_ref, returned_4, select_4, scale, final_ref, buffer, sems):
@@ -491,20 +497,23 @@
             pltpu.VMEM((RING, 2, top, local_tokens), jnp.int32),
             pltpu.VMEM((RING, 2, RING, local_tokens), jnp.float32),
             dma((2,)),
+            dma(()),
             dma((2, 7)),
+            dma(()),
             dma((2, 7)),
+            dma(()),
+            dma(()),
             dma((2, 7)),
+            dma(()),
             dma((2, 7)),
             dma(()),
             dma(()),
-            dma((2, 7)),
-            dma((2, 7)),
-            dma((2, 7)),
-            dma((2, 7)),
-            dma((RING, 2)),
-            dma((RING, 2)),
-            dma((len(GROUPS), RING, 2)),
-            dma((len(GROUPS), RING, 2)),
+            dma(()),
+            dma(()),
+            dma((len(GROUPS),)),
+            dma((len(GROUPS),)),
+            dma((len(GROUPS),)),
+            dma((len(GROUPS),)),
         ],
         compiler_params=pltpu.CompilerParams(
             collective_id=0, has_side_effects=True, vmem_limit_bytes=52 * 2**20

time: 113 us -> 109 us (0.965)
  Pallas kernels: 113 us -> 109 us
    pallas_call x1, Pallas kernels: 112 us -> 107 us  [shards(): pl.pallas_call(kernel, out_shape=(pltpu.VMEM((choices, 2 * hidden), bf16)...]
where the time goes in v3:
time: 109 us
  Pallas kernels  109 us (100%)
    pallas_call x1, Pallas kernels, shards(): pl.pallas_call(kernel, out_shape=(pltpu.VMEM((choices, 2 * hidden), bf16)...  107 us

profile of v3, /device:TPU:1, one launch (start us, length us, event | category | flops | bytes accessed | tf_op | source)
XLA Modules:
  0.0 108.7 jit_solution(16868415206318617231)
XLA Ops:
  0.0 107.2 %shard_map.46 = (bf16[1024,768]{1,0:T(8,128)(2,1)S(1)}, bf16[2,8,24,384]{3,2,1,0:T(8,128)(2,1)S(1)}, bf16[1024,192]{1,0:T(8,128)(2,1)S(1)}, f32[1024,128]{1,0:T(8,128)S(1)}) custom-call(bf16[384,2048]{1,0:T(8,128)(2,1)} %down_ref.1, bf16[128,2048]{1,0:T(8,128)(2,1)} %grad_ref.1, s32[8,128]{1,0:T(8,128)} %bitcast.3, f32[8,128]{1,0:T(8,128)} %bitcast.4), custom_call_target="tpu_custom_call" | custom-call | tf_op jit(solution)/shard_map/pallas_call | solution.py:480
  107.2 1.5 %shard_map.47 = bf16[1024,768]{1,0:T(8,128)(2,1)} custom-call(bf16[1024,768]{1,0:T(8,128)(2,1)S(1)} %get-tuple-element.9.out_ref, bf16[2,8,24,384]{3,2,1,0:T(8,128)(2,1)S(1)} %get-tuple-element.10.returned_4, bf16[1024,192]{1,0:T(8,128)(2,1)S(1)} %get-tuple-element.11.select_4, f32[1024,128]{1,0:T(8,128)S(1)} %get-tuple-element.12.scale), custom_call_target="tpu_custom_call" | custom-call | tf_op jit(solution)/shard_map/pallas_call | solution.py:523

commit v4 on v3

--- a/solution.py
+++ b/solution.py
@@ -231,11 +231,28 @@
         both = jnp.concatenate(products, axis=1) if len(products) > 1 else products[0]
         outgoing[group][2 * first : 2 * last] = both.astype(bf16)
 
+    def keep_own(group):
+        returned[group][core, 0] = outgoing[group][core]
+
+    def send_in_z_order(group):
+        for dest in range(RING):
+            rel = (dest - z + RING) % RING
+
+            @pl.when(rel != 0)
+            def _():
+                for c in range(2):
+                    send(
+                        outgoing[group].at[2 * position_of(rel) + c],
+                        returned[group].at[core, position_of((RING - rel) % RING)],
+                        b_send.at[group],
+                        b_recv.at[group],
+                        at_z(rel, c),
+                    )
+
     def send_back(group, positions):
         for q in positions:
             rel = REL[q]
             if q == 0:
-                returned[group][core, 0] = outgoing[group][core]
                 send(
                     outgoing[group].at[other],
                     returned[group].at[core, 0],
@@ -400,6 +417,7 @@
     z_event(5)
     y_event(3)
     multiply(0, 0, 5)
+    keep_own(0)
     send_back(0, (3, 4, 1, 2, 0))
     partner_event(4)
     partner_event(5)
@@ -417,8 +435,10 @@
     x_event(2)
     x_event(3)
     multiply(1, 0, 8)
+    keep_own(1)
     send_back(1, order)
     multiply(2, 0, 8)
+    keep_own(2)
     send_back(2, order)
     y_event(5)
     y_event(6)
@@ -426,11 +446,14 @@
     assemble(0)
     x_event(5)
     multiply(3, 0, 8)
+    keep_own(3)
     send_back(3, order)
     assemble(1)
     x_event(6)
     multiply(4, 0, 8)
-    send_back(4, order)
+    keep_own(4)
+    send_in_z_order(4)
+    send_back(4, (0,))
     assemble(2)
     assemble(3)
     await_returned(4)

time: 109 us -> 107 us (0.982)
  Pallas kernels: 109 us -> 107 us
    pallas_call x1, Pallas kernels: 107 us -> 105 us  [shards(): pl.pallas_call(kernel, out_shape=(pltpu.VMEM((choices, 2 * hidden), bf16)...]
where the time goes in v4:
time: 107 us
  Pallas kernels  107 us (100%)
    pallas_call x1, Pallas kernels, shards(): pl.pallas_call(kernel, out_shape=(pltpu.VMEM((choices, 2 * hidden), bf16)...  105 us

profile of v4, /device:TPU:1, one launch (start us, length us, event | category | flops | bytes accessed | tf_op | source)
XLA Modules:
  0.0 106.7 jit_solution(16517509563247011423)
XLA Ops:
  0.0 105.1 %shard_map.46 = (bf16[1024,768]{1,0:T(8,128)(2,1)S(1)}, bf16[2,8,24,384]{3,2,1,0:T(8,128)(2,1)S(1)}, bf16[1024,192]{1,0:T(8,128)(2,1)S(1)}, f32[1024,128]{1,0:T(8,128)S(1)}) custom-call(bf16[384,2048]{1,0:T(8,128)(2,1)} %down_ref.1, bf16[128,2048]{1,0:T(8,128)(2,1)} %grad_ref.1, s32[8,128]{1,0:T(8,128)} %bitcast.3, f32[8,128]{1,0:T(8,128)} %bitcast.4), custom_call_target="tpu_custom_call" | custom-call | tf_op jit(solution)/shard_map/pallas_call | solution.py:503
  105.1 1.5 %shard_map.47 = bf16[1024,768]{1,0:T(8,128)(2,1)} custom-call(bf16[1024,768]{1,0:T(8,128)(2,1)S(1)} %get-tuple-element.9.out_ref, bf16[2,8,24,384]{3,2,1,0:T(8,128)(2,1)S(1)} %get-tuple-element.10.returned_4, bf16[1024,192]{1,0:T(8,128)(2,1)S(1)} %get-tuple-element.11.select_4, f32[1024,128]{1,0:T(8,128)S(1)} %get-tuple-element.12.scale), custom_call_target="tpu_custom_call" | custom-call | tf_op jit(solution)/shard_map/pallas_call | solution.py:546

commit v5 on v4

--- a/solution.py
+++ b/solution.py
@@ -116,8 +116,8 @@
     load_wts.start()
 
     barrier = pltpu.get_barrier_semaphore()
-    peers = [partner, at_y(1), at_y(-1 + RING), at_x(1), at_x(-1 + X_RING)]
-    peers += [at_z(rel, c) for rel in range(1, RING) for c in range(2)]
+    peers = [partner, at_y(1), at_y(RING - 1), at_x(1), at_x(X_RING - 1)]
+    peers += [at_z(1, core), at_z(RING - 1, core)]
     for peer in peers:
         pl.semaphore_signal(barrier, inc=1, device_id=peer, device_id_type=MESH)
     pl.semaphore_wait(barrier, len(peers))
@@ -141,6 +141,16 @@
             at_z(hop, core),
         )
 
+    def routes_send(direction, d):
+        src, dst, hop = (-d, -d - 1, 1) if direction == 0 else (d, d + 1, RING - 1)
+        send(
+            routes_all.at[POS[src % RING], core] if d else routes_t_ref,
+            routes_all.at[POS[dst % RING], core],
+            r_send,
+            r_recv.at[direction, d],
+            at_z(hop, core),
+        )
+
     def z_arrival(direction, k):
         d = k // 2
         return (-d - 1, k % 2) if direction == 0 else (d + 1, 1 - k % 2)
@@ -148,6 +158,19 @@
     def z_event(k):
         for direction in range(2):
             chunk = z_arrival(direction, k)
+            d = k // 2
+            if k % 2 == 0 and d + direction < 4:
+                spot = POS[chunk[0] % RING]
+                await_copy(routes_all.at[spot, core], r_recv.at[direction, d])
+                if d + 1 + direction < 4:
+                    routes_send(direction, d + 1)
+                send(
+                    routes_all.at[spot, core],
+                    routes_all.at[spot, core],
+                    rp_send,
+                    rp_recv.at[direction, d],
+                    partner,
+                )
             await_copy(tok_chunk(*chunk), tz_recv.at[direction, k])
             if k <= 4:
                 z_send(direction, k + 2)
@@ -161,7 +184,10 @@
 
     def partner_event(k):
         for direction in range(2):
-            await_copy(tok_chunk(*z_arrival(direction, k), other), tp_recv.at[direction, k])
+            rel, half = z_arrival(direction, k)
+            if k % 2 == 0 and k // 2 + direction < 4:
+                await_copy(routes_all.at[POS[rel % RING], other], rp_recv.at[direction, k // 2])
+            await_copy(tok_chunk(rel, half, other), tp_recv.at[direction, k])
 
     base = 2 * (x % 2)
 
@@ -349,67 +375,62 @@
 
         lax.fori_loop(0, top, body, 0)
 
-    def source_slots():
+    def source_slots(q):
         sub = lax.broadcasted_iota(jnp.int32, (RING, local_tokens), 0)
         expert = z * RING + ((y + rel_of(sub)) & 7)
         named = []
-        for q in range(RING):
-            for s in range(2):
-                value = jnp.zeros((RING, local_tokens), f32)
-                for j in range(RING):
-                    value = jnp.where(routes_all[q, s, j : j + 1, :] == expert, 1.0, value)
-                named.append(value)
+        for s in range(2):
+            value = jnp.zeros((RING, local_tokens), f32)
+            for j in range(RING):
+                value = jnp.where(routes_all[q, s, j : j + 1, :] == expert, 1.0, value)
+            named.append(value)
         named = jnp.concatenate(named, axis=0)
         a = lax.broadcasted_iota(jnp.int32, (local_tokens, local_tokens), 0)
         b = lax.broadcasted_iota(jnp.int32, (local_tokens, local_tokens), 1)
         before = jnp.where(a < b, 1.0, 0.0).astype(bf16)
         counts = jnp.dot(named.astype(bf16), before, preferred_element_type=f32)
         row = lax.broadcasted_iota(jnp.int32, named.shape, 0)
-        counts = counts + jnp.where((row >> 3) & 1 == 1, float(CAP), 0.0)
-        slots_all[...] = jnp.where(named > 0.5, counts, -1.0).reshape(slots_all.shape)
-
-    for rel in (4, 3, 5, 2, 6, 1, 7):
-        for c in range(2):
-            send(
-                routes_t_ref,
-                routes_all.at[POS[RING - rel], core],
-                r_send,
-                r_recv,
-                at_z(rel, c),
-            )
-    send(routes_t_ref, routes_all.at[0, core], rp_send, rp_recv, partner)
+        counts = counts + jnp.where(row >= RING, float(CAP), 0.0)
+        slots_all[q] = jnp.where(named > 0.5, counts, -1.0).reshape(slots_all.shape[1:])
+
     load_tok.wait()
+    for direction in range(2):
+        routes_send(direction, 0)
     for k in range(2):
         for direction in range(2):
             z_send(direction, k)
+    send(routes_t_ref, routes_all.at[0, core], rp_send, own_recv.at[0], partner)
     load_wts.wait()
     for k in range(2):
         for direction in range(2):
             y_send(direction, k)
-    send(tok.at[0, own_rows], tok.at[0, own_rows], tp_send, own_recv, partner)
+    send(tok.at[0, own_rows], tok.at[0, own_rows], tp_send, own_recv.at[1], partner)
     routes_all[0, core] = routes_t_ref[...]
 
     home_selection()
-    await_copy(routes_all.at[0, other], rp_recv)
-    await_copy(routes_all.at[1:RING], r_recv)
-    source_slots()
+    await_copy(routes_all.at[0, other], own_recv.at[0])
     other_rows = pl.ds(pl.multiple_of(other * local_tokens, local_tokens), local_tokens)
-    await_copy(tok.at[0, other_rows], own_recv)
+    await_copy(tok.at[0, other_rows], own_recv.at[1])
+    source_slots(0)
     z_event(0)
     gather(0)
     y_event(0)
     z_event(1)
     partner_event(0)
     partner_event(1)
+    source_slots(1)
     gather(1)
+    source_slots(2)
     gather(2)
     z_event(2)
     y_event(1)
     z_event(3)
     partner_event(2)
     partner_event(3)
+    source_slots(3)
     gather(3)
     y_event(2)
+    source_slots(4)
     gather(4)
     z_event(4)
     x_event(0)
@@ -421,12 +442,15 @@
     send_back(0, (3, 4, 1, 2, 0))
     partner_event(4)
     partner_event(5)
+    source_slots(5)
     gather(5)
+    source_slots(6)
     gather(6)
     multiply(0, 5, 7)
     send_back(0, (5, 6))
     z_event(6)
     partner_event(6)
+    source_slots(7)
     gather(7)
     multiply(0, 7, 8)
     send_back(0, (7,))
@@ -461,8 +485,8 @@
     await_copy(tok.at[:, 0:local_tokens], tp_send)
     await_copy(wts.at[0 : RING - 1, 0 : hidden // 2], wy_send)
     await_copy(wts.at[0 : RING - 1, 0 : hidden // 2], wx_send)
-    await_copy(routes_all.at[1:RING], r_send)
-    await_copy(routes_all.at[0, other], rp_send)
+    await_copy(routes_all.at[0 : RING - 1, 0], r_send)
+    await_copy(routes_all.at[:, 0], rp_send)
     for group in range(len(GROUPS)):
         await_copy(outgoing[group].at[2 : 2 * RING], b_send.at[group])
         await_copy(outgoing[group].at[other], bp_send.at[group])
@@ -524,15 +548,15 @@
             dma((2, 7)),
             dma(()),
             dma((2, 7)),
-            dma(()),
+            dma((2,)),
             dma(()),
             dma((2, 7)),
             dma(()),
             dma((2, 7)),
             dma(()),
+            dma((2, 4)),
             dma(()),
-            dma(()),
-            dma(()),
+            dma((2, 4)),
             dma((len(GROUPS),)),
             dma((len(GROUPS),)),
             dma((len(GROUPS),)),

time: 107 us -> 108 us (level)
  no operation moved by 1% of the time
where the time goes in v5:
time: 108 us
  Pallas kernels  108 us (100%)
    pallas_call x1, Pallas kernels, shards(): pl.pallas_call(kernel, out_shape=(pltpu.VMEM((choices, 2 * hidden), bf16)...  106 us

profile of v5, /device:TPU:1, one launch (start us, length us, event | category | flops | bytes accessed | tf_op | source)
XLA Modules:
  0.0 107.7 jit_solution(14359576444734325287)
XLA Ops:
  0.0 106.1 %shard_map.46 = (bf16[1024,768]{1,0:T(8,128)(2,1)S(1)}, bf16[2,8,24,384]{3,2,1,0:T(8,128)(2,1)S(1)}, bf16[1024,192]{1,0:T(8,128)(2,1)S(1)}, f32[1024,128]{1,0:T(8,128)S(1)}) custom-call(bf16[384,2048]{1,0:T(8,128)(2,1)} %down_ref.1, bf16[128,2048]{1,0:T(8,128)(2,1)} %grad_ref.1, s32[8,128]{1,0:T(8,128)} %bitcast.3, f32[8,128]{1,0:T(8,128)} %bitcast.4), custom_call_target="tpu_custom_call" | custom-call | tf_op jit(solution)/shard_map/pallas_call | solution.py:527
  106.1 1.5 %shard_map.47 = bf16[1024,768]{1,0:T(8,128)(2,1)} custom-call(bf16[1024,768]{1,0:T(8,128)(2,1)S(1)} %get-tuple-element.9.out_ref, bf16[2,8,24,384]{3,2,1,0:T(8,128)(2,1)S(1)} %get-tuple-element.10.returned_4, bf16[1024,192]{1,0:T(8,128)(2,1)S(1)} %get-tuple-element.11.select_4, f32[1024,128]{1,0:T(8,128)S(1)} %get-tuple-element.12.scale), custom_call_target="tpu_custom_call" | custom-call | tf_op jit(solution)/shard_map/pallas_call | solution.py:570
